TPU v7x, 32 devices: a whole 2x2x4 slice. The times are simulated.
32 devices in a mesh: band: 16 (over z, y, core), spin: 2 (over x).
Axes of the slice: x: 2, y: 2, z: 4, core: 2. Of those that a mesh axis runs over, the one named last changes fastest.
Arguments:
- coefficients: bfloat16 [2, 2, 32, 524288], P('spin', None, 'band'), may hold values from -1 to 1
- occupation: int32 [2, 32], P('spin', 'band'), may hold values from 0 to 1000
- miller: int32 [3, 524288], P(None, ('band', 'spin')), may hold values from -8 to 8
- density: float32 [2, 256, 128, 128], P('spin', 'band'), may hold values from 0.25 to 2
- local_factor: float32 [2, 256, 128, 128], P(None, None, 'band'), may hold values from -1.2 to 1.2
Outputs:
- stress: float32 [6], replicated
- kinetic_density: float32 [524288], P(('band', 'spin'))
- gradient_square: float32 [2, 256, 128, 128], P('spin', 'band')
All inputs are finite; a program needn't handle non-finite values.
Results may differ from a plain program's by a relative error of at most 0.0003.
Values sent between devices are 32-bit elements; how exact they have to be, the bound alone decides.
No kernel may reach another device: no remote copies, remote signals or barrier semaphores. Data moves between devices by JAX's collectives and lax.ppermute only.
A program may use at most 64 MiB of HBM per device.

v0:
```python
import numpy as np
import jax
import jax.numpy as jnp
from jax import lax
from jax.sharding import PartitionSpec as P

occupation_unit = 1000.0
kpoint = (0.25, 0.125, 0.375)
spacing = 0.25
HIGH = lax.Precision.HIGH


def derivative_table(length):
    wrapped = np.mod(np.arange(length)[:, None] - np.arange(length)[None, :], length)
    angles = np.pi / length * wrapped
    sines = np.where(wrapped == 0, 1.0, np.sin(angles))
    parity = 1.0 - 2.0 * (wrapped % 2)
    return np.where(wrapped == 0, 0.0, 0.5 * parity * np.cos(angles) / sines).astype(np.float32)


def fourier_tables(length):
    phases = np.mod(np.arange(length)[:, None] * np.arange(length)[None, :], length) * (
        2.0 * np.pi / length
    )
    return (np.cos(phases), np.sin(phases))


def frequencies(length):
    positions = np.arange(length)
    signed = np.where(positions >= length // 2, positions - length, positions)
    return (2.0 * np.pi / length * signed).astype(np.float32)


def halves(values, axis, mine):
    return (
        lax.dynamic_index_in_dim(values, mine, axis, keepdims=False),
        lax.dynamic_index_in_dim(values, 1 - mine, axis, keepdims=False),
    )


def pair_up(size, bit):
    return [(i, i ^ bit) for i in range(size)]


def scatter_sum(values, band_devices, band, spin):
    tail = values.shape[2:]
    spins = values.shape[1]
    bit = 1
    left = band_devices
    done_spin = False
    rest = values.reshape((left, spins) + tail)
    while left > 1:
        mine = band // bit % 2
        rest = rest.reshape((left // 2, 2) + rest.shape[1:])
        keep, give = halves(rest, 1, mine)
        rest = keep + lax.ppermute(give, "band", pair_up(band_devices, bit))
        left //= 2
        bit *= 2
        if not done_spin:
            keep, give = halves(rest, 1, spin)
            rest = keep + lax.ppermute(give, "spin", pair_up(spins, 1))
            done_spin = True
    return rest.reshape(tail)


def shards(coefficients, occupation, miller, density, local_factor):
    band_devices = lax.axis_size("band")
    spins = lax.axis_size("spin")
    band = lax.axis_index("band")
    spin = lax.axis_index("spin")
    planes, nx, ny = density.shape[1:]
    nz = planes * band_devices
    rows = nx // band_devices
    cell_count = nz * nx * ny
    waves = coefficients.shape[3]
    dens = density[0]
    dens_send = dens.reshape(planes, band_devices, rows, ny).transpose(1, 0, 2, 3)
    dens_col = lax.all_to_all(dens_send, "band", 0, 0, tiled=True).reshape(nz, rows * ny)
    share = planes // spins
    keep, give = halves(dens.reshape(spins, share, nx, ny), 0, spin)
    total = keep + lax.ppermute(give, "spin", pair_up(spins, 1))
    weights = occupation[0].astype(jnp.float32) / occupation_unit
    piece = coefficients[0].astype(jnp.float32)
    partial = jnp.sum((piece[0] * piece[0] + piece[1] * piece[1]) * weights[:, None], axis=0)
    chunk = waves // (band_devices * spins)
    kinetic_weight = scatter_sum(
        partial.reshape(band_devices, spins, chunk // 128, 128), band_devices, band, spin
    )
    cos_x, sin_x = fourier_tables(nx)
    cos_y, sin_y = fourier_tables(ny)
    cos_z, sin_z = fourier_tables(nz)
    part = ny // spins
    table_y = np.stack(
        [
            np.stack(
                [
                    np.concatenate([cos_y[:, p : p + part], -sin_y[:, p : p + part]], 1),
                    np.concatenate([-sin_y[:, p : p + part], -cos_y[:, p : p + part]], 1),
                ]
            )
            for p in range(0, ny, part)
        ]
    ).astype(np.float32)
    along = jnp.einsum("zxj,pcjm->pczxm", total, table_y, precision=HIGH)
    table_x = np.stack([cos_x, sin_x]).reshape(2, band_devices, rows, nx).astype(np.float32)
    plane = jnp.einsum("cbrj,pczjm->bpzrm", table_x, along, precision=HIGH)
    lanes = plane.shape[-1]
    plane = plane.reshape(band_devices * spins, share, rows, lanes)
    column = lax.all_to_all(plane, ("band", "spin"), 0, 0, tiled=True).reshape(nz, rows * lanes)
    gradz_col = jnp.dot(derivative_table(nz), dens_col, precision=HIGH)
    gradz_back = lax.all_to_all(
        gradz_col.reshape(band_devices, planes, rows, ny), "band", 0, 0, tiled=True
    )
    grad_z = gradz_back.transpose(1, 0, 2, 3).reshape(planes, nx, ny)
    first = jnp.dot((cos_z / cell_count).astype(np.float32), column, precision=HIGH).reshape(
        nz, rows, lanes
    )
    second = jnp.dot((sin_z / cell_count).astype(np.float32), column, precision=HIGH).reshape(
        nz, rows, lanes
    )
    spectrum = first + jnp.concatenate([second[..., part:], -second[..., :part]], axis=-1)
    factor = lax.dynamic_slice_in_dim(local_factor, spin * part, part, 3)
    factor = jnp.concatenate([factor[0], factor[1]], axis=-1)
    freq_z = jnp.asarray(frequencies(nz))[:, None, None]
    freq_x = lax.dynamic_slice_in_dim(jnp.asarray(frequencies(nx)), band * rows, rows, 0)[:, None]
    freq_y = lax.dynamic_slice_in_dim(jnp.asarray(frequencies(ny)), spin * part, part, 0)
    freq_y = jnp.concatenate([freq_y, freq_y])[None, :]
    length_sq = freq_x * freq_x + freq_y * freq_y + freq_z * freq_z
    positive = length_sq > 0
    inverse = jnp.where(positive, 1.0 / jnp.where(positive, length_sq, 1.0), 0.0)
    hartree = 4.0 * np.pi * spectrum * spectrum * inverse
    both = 2.0 * (hartree * inverse + spectrum * factor)
    trace = jnp.sum(hartree, axis=0)
    sum_0 = jnp.sum(both, axis=0)
    sum_1 = jnp.sum(both * freq_z, axis=0)
    sum_2 = jnp.sum(both * (freq_z * freq_z), axis=0)
    recip = [
        sum_0 * freq_x * freq_x - trace,
        sum_0 * freq_y * freq_y - trace,
        sum_2 - trace,
        sum_1 * freq_y,
        sum_1 * freq_x,
        sum_0 * freq_x * freq_y,
    ]
    recip = [jnp.sum(r, axis=0) for r in recip]
    deriv_x = derivative_table(nx)
    deriv_y = derivative_table(ny)
    grad_x = jnp.einsum("ik,zky->ziy", deriv_x, dens, precision=HIGH)
    grad_y = jnp.einsum("zxk,ik->zxi", dens, deriv_y, precision=HIGH)
    square = grad_x * grad_x + grad_y * grad_y + grad_z * grad_z
    kernel = dens ** (-1.0 / 3.0) / (1.0 + square / (4.0 * dens * dens + 1.0)) * (-1.0 / cell_count)

    def six(weighting, a, b, c, axes):
        wa, wb = (weighting * a, weighting * b)
        return [
            jnp.sum(v, axis=axes)
            for v in (wa * a, wb * b, weighting * c * c, wb * c, wa * c, wa * b)
        ]

    xc = six(kernel, grad_x, grad_y, grad_z, (0, 1))
    kvec = jnp.array(kpoint, jnp.float32)
    gvec = spacing * (
        miller.reshape(3, chunk // 128, 128).astype(jnp.float32) + kvec[:, None, None]
    )
    kinetic_density = 0.5 * (gvec[0] ** 2 + gvec[1] ** 2 + gvec[2] ** 2) * kinetic_weight
    kinetic = six(kinetic_weight * (-1.0 / waves), gvec[0], gvec[1], gvec[2], 0)
    lanewise = jnp.stack([r + x + k for r, x, k in zip(recip, xc, kinetic)])
    stress = jnp.sum(lax.psum(lanewise, ("band", "spin")), axis=1)
    return (stress, kinetic_density.reshape(chunk), square[None])


def solution(mesh):
    return jax.shard_map(
        shards,
        mesh=mesh,
        in_specs=(
            P("spin", None, "band", None),
            P("spin", "band"),
            P(None, ("band", "spin")),
            P("spin", "band", None, None),
            P(None, None, "band", None),
        ),
        out_specs=(P(), P(("band", "spin")), P("spin", "band", None, None)),
        check_vma=False,
    )
```

profile of v0, /device:TPU:0, one launch (start us, length us, event | category | flops | bytes accessed | tf_op | source)
XLA Modules:
  0.0 179.8 jit_solution(8025798165100008383)
XLA Ops:
  0.6 2.3 %copy_bitcast_fusion = f32[16,16,8,128]{3,2,1,0:T(8,128)} fusion(f32[1,16,128,128]{3,2,1,0:T(8,128)} %param.19), kind=kLoop, calls=%fused_computation.46 | loop fusion | bytes 2097152 | tf_op jit(solution)/shard_map/transpose | solution.py:77
  2.9 7.5 %all-to-all-start.1 = ((f32[16,16,8,128]{3,2,1,0:T(8,128)}), f32[16,16,8,128]{3,2,1,0:T(8,128)}, u32[]{:S(2)}, u32[]{:S(2)}) async-start(f32[16,16,8,128]{3,2,1,0:T(8,128)} %copy_bitcast_fusion), calls=%async_computation.1 | async-start | bytes 2097152 | tf_op jit(solution)/shard_map/all_to_all | solution.py:78
  10.4 0.0 copy-start.15
  10.4 6.6 %convert_element_type.18 = f32[1,2,2,524288]{3,2,1,0:T(2,128)} convert(bf16[1,2,2,524288]{3,2,1,0:T(2,128)(2,1)} %param.16) | non-fusion elementwise | flops 2097152 | bytes 12582912 | tf_op jit(solution)/shard_map/convert_element_type | solution.py:83
  17.1 23.5 %fusion.3 = f32[524288]{0:T(1024)S(1)} fusion(f32[1,2,2,524288]{3,2,1,0:T(2,128)} %convert_element_type.18, f32[2]{0:T(128)S(1)} %multiply_bitcast_fusion.1), kind=kLoop, calls=%fused_computation.5 | loop fusion | flops 4718592 | bytes 10485768 | tf_op jit(solution)/shard_map/reduce_sum | solution.py:84
  40.5 0.0 copy-start
  40.6 0.0 copy-start.13
  40.6 0.0 copy-start.8
  40.6 1.0 dynamic-slice_bitcast_fusion.2
  41.6 0.3 collective-permute-start.1
  42.0 0.2 copy-done
  42.2 0.9 dynamic-slice_bitcast_fusion.4
  43.0 1.5 collective-permute-start
  44.5 0.1 dynamic_slice.50
  44.6 0.1 pad_maximum_fusion.2
  44.7 0.1 fusion.49
  44.7 0.7 convert_bitcast_fusion
  45.5 0.1 add.324
  45.6 1.4 bitcast_add_fusion
  47.0 0.0 copy-start.1
  47.0 0.0 copy-start.9
  47.0 0.8 dynamic-slice_bitcast_fusion.3
  47.8 0.6 collective-permute-start.2
  48.4 9.7 %collective-permute-done = f32[8,128,128]{2,1,0:T(8,128)} collective-permute-done((f32[8,128,128]{2,1,0:T(8,128)}, f32[8,128,128]{2,1,0:T(8,128)}, u32[]{:S(2)}, u32[]{:S(2)}) %collective-permute-start) | collective-permute-done | bytes 524320 | tf_op jit(solution)/shard_map/ppermute | solution.py:81
  58.1 2.0 %fusion.29 = f32[8,128,2,2,128]{4,1,3,0,2:T(8,128)S(1)} fusion(f32[2,2,128,128,1]{3,2,1,4,0:T(8,128)S(1)} %copy-done.7, f32[8,128,128]{2,1,0:T(8,128)} %collective-permute-done, f32[2,8,128,128]{3,2,1,0:T(8,128)S(1)} %bitcast.248, s32[]{:T(128)S(6)} %select_n.90), kind=kOutput, calls=%fused_computation.58 | convolution fusion | flops 402784256 | bytes 3407876 | tf_op jit(solution)/shard_map/zxj,pcjm->pczxm/dot_general | solution.py:104
  60.1 0.7 fusion.6
  60.9 0.0 copy-start.14
  60.9 0.0 copy-start.2
  60.9 1.4 copy.33
  62.3 6.2 %all-to-all-start = ((f32[32,8,8,128]{3,2,1,0:T(8,128)}), f32[32,8,8,128]{3,2,1,0:T(8,128)}, u32[]{:S(2)}, u32[]{:S(2)}) async-start(f32[32,8,8,128]{3,2,1,0:T(8,128)} %bitcast.15), calls=%async_computation | async-start | bytes 2097152 | tf_op jit(solution)/shard_map/all_to_all | solution.py:109
  68.5 0.1 fusion.32
  68.6 0.0 collective-permute-done.2
  68.6 0.1 bitcast_add_fusion.1
  68.7 1.7 collective-permute-start.3
  70.4 1.6 convolution_bitcast_fusion.1
  72.0 13.8 %collective-permute-done.3 = f32[4,128,128]{2,1,0:T(8,128)S(1)} collective-permute-done((f32[4,128,128]{2,1,0:T(8,128)S(1)}, f32[4,128,128]{2,1,0:T(8,128)S(1)}, u32[]{:S(2)}, u32[]{:S(2)}) %collective-permute-start.3) | collective-permute-done | bytes 262176 | tf_op jit(solution)/shard_map/ppermute | solution.py:56
  85.9 1.3 collective-permute-start.4
  87.2 0.6 dynamic-slice_bitcast_fusion.1
  87.8 4.9 %collective-permute-done.4 = f32[2,128,128]{2,1,0:T(8,128)S(1)} collective-permute-done((f32[2,128,128]{2,1,0:T(8,128)S(1)}, f32[2,128,128]{2,1,0:T(8,128)S(1)}, u32[]{:S(2)}, u32[]{:S(2)}) %collective-permute-start.4) | collective-permute-done | bytes 131104 | tf_op jit(solution)/shard_map/ppermute | solution.py:56
  92.7 0.6 constant_dynamic-slice_fusion
  93.3 2.5 %collective-permute-start.5 = (f32[1,128,128]{2,1,0:T(8,128)}, f32[1,128,128]{2,1,0:T(8,128)}, u32[]{:S(2)}, u32[]{:S(2)}) collective-permute-start(f32[1,128,128]{2,1,0:T(8,128)} %constant_dynamic-slice_fusion), channel_id=1, source_target_pairs={{0,16},{2,18},{4,20},{6,22},{8,24},{10,26},{12,28},{14,30},{16,0},... | collective-permute-start | bytes 196616 | tf_op jit(solution)/shard_map/ppermute | solution.py:56
  95.8 2.4 %copy.72 = f32[32,8,8,128]{3,1,2,0:T(8,128)} copy(f32[32,8,8,128]{3,2,1,0:T(8,128)} %bitcast.80) | data formatting | bytes 2097152
  98.2 2.5 %copy.35 = f32[1024,256]{1,0:T(8,128)} copy(f32[1024,256]{0,1:T(8,128)} %bitcast.252) | data formatting | bytes 2097152 | tf_op jit(solution)/shard_map/dot_general | solution.py:110
  100.8 2.9 %fusion.50 = f32[16,16,8,128]{3,1,2,0:T(8,128)} fusion(f32[16,16,256,1]{2,1,3,0:T(8,128)} %constant.184, f32[8,128,256,1]{2,1,0,3:T(8,128)} %bitcast.251), kind=kOutput, calls=%fused_computation.118 | convolution fusion | flops 402653184 | bytes 2359296 | tf_op jit(solution)/shard_map/dot_general | solution.py:110
  103.7 4.3 %all-to-all-start.2 = ((f32[16,16,8,128]{3,1,2,0:T(8,128)}), f32[16,16,8,128]{3,1,2,0:T(8,128)}, u32[]{:S(2)}, u32[]{:S(2)}) async-start(f32[16,16,8,128]{3,1,2,0:T(8,128)} %fusion.50), calls=%async_computation.2 | async-start | bytes 2097152 | tf_op jit(solution)/shard_map/all_to_all | solution.py:111
  108.0 1.3 pad_maximum_fusion.1
  109.3 1.5 multiply_bitcast_fusion
  110.8 0.1 fusion.37
  110.9 2.0 %convolution_bitcast_fusion.2 = f32[32,8,8,128]{3,1,2,0:T(8,128)S(1)} fusion(f32[256,256]{1,0:T(8,128)} %constant.168.clone, f32[32,8,8,128]{3,2,1,0:T(8,128)} %all-to-all-done), kind=kOutput, calls=%fused_computation.16 | convolution fusion | flops 402653184 | bytes 2359296 | tf_op jit(solution)/shard_map/dot_general | solution.py:118
  112.9 0.2 copy.44
  113.1 0.3 fusion.48
  113.5 0.0 copy-start.16
  113.5 0.0 copy-start.17
  113.5 0.3 pad_maximum_fusion
  113.9 0.8 copy-done.5
  114.7 0.0 copy-done.16
  114.8 2.5 %fusion.17 = (f32[256,1024]{1,0:T(8,128)S(1)}, f32[1024]{0:T(1024)S(1)}) fusion(f32[32,8,8,128]{3,2,1,0:T(8,128)S(1)} %bitcast.255, f32[256]{0:T(256)S(1)} %copy-done.17, f32[1024]{0:T(1024)S(1)} %bitcast_add_fusion.7, f32[32,8,8,128]{3,2,1,0:T(8,128)S(1)} %bitcast.256, f32[256,256]{1,0:T(8,128)S(1)} %copy-done.16, f32[32,8,8,128]{3,2,1,0:T(8,128)} %all-to-all-done), kind=kOutput, calls=%fused_computation.28 | convolution fusion | flops 406060032 | bytes 4465664 | tf_op jit(solution)/shard_map/dot_general | solution.py:115
  117.3 0.3 multiply_reduce_fusion.1
  117.6 0.1 fusion.43
  117.7 13.2 %all-to-all-done.2 = f32[16,16,8,128]{3,1,2,0:T(8,128)} async-done(((f32[16,16,8,128]{3,1,2,0:T(8,128)}), f32[16,16,8,128]{3,1,2,0:T(8,128)}, u32[]{:S(2)}, u32[]{:S(2)}) %all-to-all-start.2) | async-done | bytes 1048608 | tf_op jit(solution)/shard_map/all_to_all | solution.py:111
  130.9 3.3 %fusion.25 = (f32[16,128,128]{2,1,0:T(8,128)S(1)}, f32[16,128,128]{2,1,0:T(8,128)S(1)}) fusion(f32[1,16,128,128]{3,2,1,0:T(8,128)S(1)} %copy-done, f32[16,16,8,128]{3,0,2,1:T(8,128)} %bitcast.33, f32[16,128,128]{2,1,0:T(8,128)S(1)} %copy-done.3, f32[128,128,1]{1,0,2:T(8,128)S(1)} %copy-done.10), kind=kOutput, calls=%fused_computation.54 | convolution fusion | flops 204472320 | bytes 5308416 | tf_op jit(solution)/shard_map/zxk,ik->zxi/dot_general | solution.py:149
  134.2 3.0 %multiply_reduce_fusion = (f32[128]{0:T(128)S(1)}, f32[128]{0:T(128)S(1)}, f32[128]{0:T(128)S(1)}, f32[128]{0:T(128)S(1)}, f32[128]{0:T(128)S(1)}, /*index=5*/f32[128]{0:T(128)S(1)}, f32[1,16,128,128]{3,2,1,0:T(8,128)}) fusion(f32[16,128,128]{2,1,0:T(8,128)S(1)} %get-tuple-element.40, f32[16,128,128]{2,1,0:T(8,128)S(1)} %get-tuple-element.39, ...), kind=kLoop, calls=%fused_computation.47 | loop fusion | flops 5242112 | bytes 5245952 | tf_op jit(solution)/shard_map/reduce_sum | solution.py:156
  137.3 41.9 %psum.7 = f32[6,128]{1,0:T(8,128)S(1)} all-reduce(f32[6,128]{1,0:T(8,128)S(1)} %stack.2), channel_id=1, replica_groups=mesh['band'=16,'spin'=2] {'band','spin'}, use_global_device_ids=true, to_apply=%region_23.24 | all-reduce | flops 768 | bytes 6144 | tf_op jit(solution)/shard_map/psum | solution.py:168
  179.2 0.6 reduce_sum.251
  (37 shorter events, 0.2 us)
Async XLA Ops:
  2.9 59.3 %all-to-all-start.1 = ((f32[16,16,8,128]{3,2,1,0:T(8,128)}), f32[16,16,8,128]{3,2,1,0:T(8,128)}, u32[]{:S(2)}, u32[]{:S(2)}) async-start(f32[16,16,8,128]{3,2,1,0:T(8,128)} %copy_bitcast_fusion), calls=%async_computation.1 | async-start | bytes 2097152 | tf_op jit(solution)/shard_map/all_to_all | solution.py:78
  10.4 6.6 %copy-start.15 = (s32[1,2]{1,0:T(1,128)S(1)}, s32[1,2]{1,0:T(1,128)}, u32[]{:S(2)}) copy-start(s32[1,2]{1,0:T(1,128)} %param.17) | copy-start | bytes 28
  40.5 1.6 copy-start
  40.6 3.9 %copy-start.13 = (f32[128]{0:T(128)S(1)}, f32[128]{0:T(128)}, u32[]{:S(2)}) copy-start(f32[128]{0:T(128)} %constant.170.clone) | copy-start | bytes 1540
  40.6 4.2 %copy-start.8 = (s32[3,16384]{1,0:T(4,128)S(1)}, s32[3,16384]{1,0:T(4,128)}, u32[]{:S(2)}) copy-start(s32[3,16384]{1,0:T(4,128)} %param.18) | copy-start | bytes 589828
  41.6 3.9 %collective-permute-start.1 = (f32[8,2,128,128]{3,2,1,0:T(8,128)}, f32[8,2,128,128]{3,2,1,0:T(8,128)}, u32[]{:S(2)}, u32[]{:S(2)}) collective-permute-start(f32[8,2,128,128]{3,2,1,0:T(8,128)} %dynamic-slice_bitcast_fusion.2), channel_id=1, source_target_pairs={{0,2},{2,0},{4,6},{6,4},{8,10},{10,8},{12,14},{14,12},{16,18},{18,... | collective-permute-start | bytes 3145736 | tf_op jit(solution)/shard_map/ppermute | solution.py:56
  43.0 15.1 %collective-permute-start = (f32[8,128,128]{2,1,0:T(8,128)}, f32[8,128,128]{2,1,0:T(8,128)}, u32[]{:S(2)}, u32[]{:S(2)}) collective-permute-start(f32[8,128,128]{2,1,0:T(8,128)} %dynamic-slice_bitcast_fusion.4), channel_id=1, source_target_pairs={{0,1},{1,0},{2,3},{3,2},{4,5},{5,4},{6,7},{7,6},{8,9},{9,8},{10,11... | collective-permute-start | bytes 1572872 | tf_op jit(solution)/shard_map/ppermute | solution.py:81
  45.6 12.6 %copy-start.7 = (f32[2,2,128,128,1]{3,2,1,4,0:T(8,128)S(1)}, f32[2,2,128,128,1]{3,2,1,4,0:T(8,128)}, u32[]{:S(2)}) copy-start(f32[2,2,128,128,1]{3,2,1,4,0:T(8,128)} %constant.181) | copy-start | bytes 786436
  47.0 1.4 copy-start.1
  47.0 13.2 %copy-start.9 = (f32[2,16,8,128,1,1]{3,1,0,2,5,4:T(8,128)S(1)}, f32[2,16,8,128,1,1]{3,1,0,2,5,4:T(8,128)}, u32[]{:S(2)}) copy-start(f32[2,16,8,128,1,1]{3,1,0,2,5,4:T(8,128)} %constant.182) | copy-start | bytes 393220
  47.8 20.8 %collective-permute-start.2 = (f32[8,128,128]{2,1,0:T(8,128)}, f32[8,128,128]{2,1,0:T(8,128)S(1)}, u32[]{:S(2)}, u32[]{:S(2)}) collective-permute-start(f32[8,128,128]{2,1,0:T(8,128)} %dynamic-slice_bitcast_fusion.3), channel_id=1, source_target_pairs={{0,1},{1,0},{2,3},{3,2},{4,5},{5,4},{6,7},{7,6},{8,9},{9,8},{10,11... | collective-permute-start | bytes 1572872 | tf_op jit(solution)/shard_map/ppermute | solution.py:61
  60.9 7.6 %copy-start.6 = (f32[1,3,128,128]{3,1,2,0:T(4,128)S(1)}, f32[1,3,128,128]{3,1,2,0:T(4,128)}, u32[]{:S(2)}) copy-start(f32[1,3,128,128]{3,1,2,0:T(4,128)} %convert_bitcast_fusion) | copy-start | bytes 589828
  60.9 7.6 %copy-start.14 = (f32[3]{0:T(128)S(1)}, f32[3]{0:T(128)}, u32[]{:S(2)}) copy-start(f32[3]{0:T(128)} %constant.172.clone) | copy-start | bytes 40
  60.9 7.7 %copy-start.2 = (f32[8,2,128,128]{3,2,1,0:T(8,128)S(1)}, f32[8,2,128,128]{3,2,1,0:T(8,128)}, u32[]{:S(2)}) copy-start(f32[8,2,128,128]{3,2,1,0:T(8,128)} %copy-done.1) | copy-start | bytes 3145732
  62.3 8.2 %copy-start.10 = (f32[128,128,1]{1,0,2:T(8,128)S(1)}, f32[128,128,1]{1,0,2:T(8,128)}, u32[]{:S(2)}) copy-start(f32[128,128,1]{1,0,2:T(8,128)} %constant.183) | copy-start | bytes 196612
  62.3 41.4 %all-to-all-start = ((f32[32,8,8,128]{3,2,1,0:T(8,128)}), f32[32,8,8,128]{3,2,1,0:T(8,128)}, u32[]{:S(2)}, u32[]{:S(2)}) async-start(f32[32,8,8,128]{3,2,1,0:T(8,128)} %bitcast.15), calls=%async_computation | async-start | bytes 2097152 | tf_op jit(solution)/shard_map/all_to_all | solution.py:109
  68.7 18.5 %copy-start.4 = (f32[2,256,8,128]{3,2,1,0:T(8,128)S(1)}, f32[2,256,8,128]{3,2,1,0:T(8,128)}, u32[]{:S(2)}) copy-start(f32[2,256,8,128]{3,2,1,0:T(8,128)} %param.20) | copy-start | bytes 6291460
  68.7 17.1 %collective-permute-start.3 = (f32[4,128,128]{2,1,0:T(8,128)S(1)}, f32[4,128,128]{2,1,0:T(8,128)S(1)}, u32[]{:S(2)}, u32[]{:S(2)}) collective-permute-start(f32[4,128,128]{2,1,0:T(8,128)S(1)} %dynamic-slice_bitcast_fusion.5), channel_id=1, source_target_pairs={{0,4},{2,6},{4,0},{6,2},{8,12},{10,14},{12,8},{14,10},{16,20},{18,... | collective-permute-start | bytes 786440 | tf_op jit(solution)/shard_map/ppermute | solution.py:56
  85.9 6.8 %collective-permute-start.4 = (f32[2,128,128]{2,1,0:T(8,128)S(1)}, f32[2,128,128]{2,1,0:T(8,128)S(1)}, u32[]{:S(2)}, u32[]{:S(2)}) collective-permute-start(f32[2,128,128]{2,1,0:T(8,128)S(1)} %dynamic-slice_bitcast_fusion.6), channel_id=1, source_target_pairs={{0,8},{2,10},{4,12},{6,14},{8,0},{10,2},{12,4},{14,6},{16,24},{18,... | collective-permute-start | bytes 393224 | tf_op jit(solution)/shard_map/ppermute | solution.py:56
  93.3 16.0 %collective-permute-start.5 = (f32[1,128,128]{2,1,0:T(8,128)}, f32[1,128,128]{2,1,0:T(8,128)}, u32[]{:S(2)}, u32[]{:S(2)}) collective-permute-start(f32[1,128,128]{2,1,0:T(8,128)} %constant_dynamic-slice_fusion), channel_id=1, source_target_pairs={{0,16},{2,18},{4,20},{6,22},{8,24},{10,26},{12,28},{14,30},{16,0},... | collective-permute-start | bytes 196616 | tf_op jit(solution)/shard_map/ppermute | solution.py:56
  103.7 27.2 %all-to-all-start.2 = ((f32[16,16,8,128]{3,1,2,0:T(8,128)}), f32[16,16,8,128]{3,1,2,0:T(8,128)}, u32[]{:S(2)}, u32[]{:S(2)}) async-start(f32[16,16,8,128]{3,1,2,0:T(8,128)} %fusion.50), calls=%async_computation.2 | async-start | bytes 2097152 | tf_op jit(solution)/shard_map/all_to_all | solution.py:111
  113.5 1.2 copy-start.5
  113.5 1.3 copy-start.16
  113.5 1.2 copy-start.17
  114.8 2.6 %copy-start.11 = (f32[256]{0:T(256)S(1)}, f32[256]{0:T(256)}, u32[]{:S(2)}) copy-start(f32[256]{0:T(256)} %constant.179) | copy-start | bytes 3076
  114.8 2.6 %copy-start.12 = (f32[256]{0:T(256)S(1)}, f32[256]{0:T(256)}, u32[]{:S(2)}) copy-start(f32[256]{0:T(256)} %constant.180) | copy-start | bytes 3076
  114.8 16.1 %copy-start.3 = (f32[16,128,128]{2,1,0:T(8,128)S(1)}, f32[16,128,128]{2,1,0:T(8,128)}, u32[]{:S(2)}) copy-start(f32[16,128,128]{2,1,0:T(8,128)} %convolution_bitcast_fusion.1) | copy-start | bytes 3145732
where the time goes:
time: 181 us; the launch traced here: 180 us
  blocking collectives  41.9 us (23%)
  waiting for transfers between devices  41.7 us (23%)
  other arithmetic  40.1 us (22%)
  starting transfers between devices  25.8 us (14%)
  matrix products  15.1 us (8%)
  local copies, waits for them, and re-layouts  14.2 us (8%)
    psum x1, blocking collectives, shards(): stress = jnp.sum(lax.psum(lanewise, ('band', 'spin')), axis=1)  41.9 us
    reduce_sum x1, other arithmetic, shards(): jnp.sum((piece[0] * piece[0] + piece[1] * piece[1]) * weights[:, None], a...  23.5 us
    ppermute x4, waiting for transfers between devices, scatter_sum(): rest = keep + lax.ppermute(give, 'band', pair_up(band_devices, bit))  18.7 us
    all_to_all x1, waiting for transfers between devices, shards(): lax.all_to_all(gradz_col.reshape(band_devices, planes, rows, ny), 'band',...  13.2 us
    ppermute x1, waiting for transfers between devices, shards(): total = keep + lax.ppermute(give, 'spin', pair_up(spins, 1))  9.74 us
    all_to_all x1, starting transfers between devices, shards(): lax.all_to_all(dens_send, 'band', 0, 0, tiled=True).reshape(nz, rows * ny)  7.46 us
    convert_element_type x1, other arithmetic, shards(): piece = coefficients[0].astype(jnp.float32)  6.6 us
    all_to_all x1, starting transfers between devices, shards(): lax.all_to_all(plane, ('band', 'spin'), 0, 0, tiled=True)  6.16 us
  transfers between devices with their start and end apart: 9, of which 4 were waited for; matrix products, arithmetic and copies ran while one was open for 33% of the time, Pallas kernels for 0%

commit v1 on v0

--- a/solution.py
+++ b/solution.py
@@ -165,7 +165,7 @@
     kinetic_density = 0.5 * (gvec[0] ** 2 + gvec[1] ** 2 + gvec[2] ** 2) * kinetic_weight
     kinetic = six(kinetic_weight * (-1.0 / waves), gvec[0], gvec[1], gvec[2], 0)
     lanewise = jnp.stack([r + x + k for r, x, k in zip(recip, xc, kinetic)])
-    stress = jnp.sum(lax.psum(lanewise, ("band", "spin")), axis=1)
+    stress = jnp.sum(jnp.sum(lax.all_gather(lanewise, ("band", "spin")), axis=0), axis=1)
     return (stress, kinetic_density.reshape(chunk), square[None])
 
 

time: 181 us -> 209 us (1.15)
  blocking collectives: 41.9 us -> 69.9 us
    all_gather x0 -> x1, blocking collectives: none -> 69.9 us  [shards(): lax.all_gather(lanewise, ('band', 'spin'))]
    psum x1 -> x0, blocking collectives: 41.9 us -> none  [shards(): stress = jnp.sum(lax.psum(lanewise, ('band', 'spin')), axis=1)]
  transfers between devices with their start and end apart: 9 -> 9, of which waited for: 4 -> 4; matrix products, arithmetic and copies ran while one was open for 33% -> 28% of each run, Pallas kernels for 0% -> 0%
where the time goes in v1:
time: 209 us; the launch traced here: 208 us
  blocking collectives  69.9 us (33%)
  waiting for transfers between devices  41.7 us (20%)
  other arithmetic  40.1 us (19%)
  starting transfers between devices  25.8 us (12%)
  matrix products  15.1 us (7%)
  local copies, waits for them, and re-layouts  14.2 us (7%)
    all_gather x1, blocking collectives, shards(): lax.all_gather(lanewise, ('band', 'spin'))  69.9 us
    reduce_sum x1, other arithmetic, shards(): jnp.sum((piece[0] * piece[0] + piece[1] * piece[1]) * weights[:, None], a...  23.5 us
    ppermute x4, waiting for transfers between devices, scatter_sum(): rest = keep + lax.ppermute(give, 'band', pair_up(band_devices, bit))  18.7 us
    all_to_all x1, waiting for transfers between devices, shards(): lax.all_to_all(gradz_col.reshape(band_devices, planes, rows, ny), 'band',...  13.2 us
    ppermute x1, waiting for transfers between devices, shards(): total = keep + lax.ppermute(give, 'spin', pair_up(spins, 1))  9.74 us
    all_to_all x1, starting transfers between devices, shards(): lax.all_to_all(dens_send, 'band', 0, 0, tiled=True).reshape(nz, rows * ny)  7.46 us
    convert_element_type x1, other arithmetic, shards(): piece = coefficients[0].astype(jnp.float32)  6.6 us
    all_to_all x1, starting transfers between devices, shards(): lax.all_to_all(plane, ('band', 'spin'), 0, 0, tiled=True)  6.16 us
  transfers between devices with their start and end apart: 9, of which 4 were waited for; matrix products, arithmetic and copies ran while one was open for 28% of the time, Pallas kernels for 0%

profile of v1, /device:TPU:0, one launch (start us, length us, event | category | flops | bytes accessed | tf_op | source)
XLA Modules:
  0.0 207.8 jit_solution(2746708768028299003)
XLA Ops:
  0.6 2.3 %copy_bitcast_fusion = f32[16,16,8,128]{3,2,1,0:T(8,128)} fusion(f32[1,16,128,128]{3,2,1,0:T(8,128)} %param.19), kind=kLoop, calls=%fused_computation.46 | loop fusion | bytes 2097152 | tf_op jit(solution)/shard_map/transpose | solution.py:77
  2.9 7.5 %all-to-all-start.1 = ((f32[16,16,8,128]{3,2,1,0:T(8,128)}), f32[16,16,8,128]{3,2,1,0:T(8,128)}, u32[]{:S(2)}, u32[]{:S(2)}) async-start(f32[16,16,8,128]{3,2,1,0:T(8,128)} %copy_bitcast_fusion), calls=%async_computation.1 | async-start | bytes 2097152 | tf_op jit(solution)/shard_map/all_to_all | solution.py:78
  10.4 0.0 copy-start.15
  10.4 6.6 %convert_element_type.18 = f32[1,2,2,524288]{3,2,1,0:T(2,128)} convert(bf16[1,2,2,524288]{3,2,1,0:T(2,128)(2,1)} %param.16) | non-fusion elementwise | flops 2097152 | bytes 12582912 | tf_op jit(solution)/shard_map/convert_element_type | solution.py:83
  17.1 23.5 %fusion.3 = f32[524288]{0:T(1024)S(1)} fusion(f32[1,2,2,524288]{3,2,1,0:T(2,128)} %convert_element_type.18, f32[2]{0:T(128)S(1)} %multiply_bitcast_fusion.1), kind=kLoop, calls=%fused_computation.5 | loop fusion | flops 4718592 | bytes 10485768 | tf_op jit(solution)/shard_map/reduce_sum | solution.py:84
  40.5 0.0 copy-start
  40.6 0.0 copy-start.13
  40.6 0.0 copy-start.8
  40.6 1.0 dynamic-slice_bitcast_fusion.2
  41.6 0.3 collective-permute-start.1
  42.0 0.2 copy-done
  42.2 0.9 dynamic-slice_bitcast_fusion.4
  43.0 1.5 collective-permute-start
  44.5 0.1 dynamic_slice.50
  44.6 0.1 pad_maximum_fusion.2
  44.7 0.1 fusion.49
  44.7 0.7 convert_bitcast_fusion
  45.5 0.1 add.322
  45.6 1.4 bitcast_add_fusion
  47.0 0.0 copy-start.1
  47.0 0.0 copy-start.9
  47.0 0.8 dynamic-slice_bitcast_fusion.3
  47.8 0.6 collective-permute-start.2
  48.4 9.7 %collective-permute-done = f32[8,128,128]{2,1,0:T(8,128)} collective-permute-done((f32[8,128,128]{2,1,0:T(8,128)}, f32[8,128,128]{2,1,0:T(8,128)}, u32[]{:S(2)}, u32[]{:S(2)}) %collective-permute-start) | collective-permute-done | bytes 524320 | tf_op jit(solution)/shard_map/ppermute | solution.py:81
  58.1 2.0 fusion.29
  60.1 0.7 fusion.6
  60.9 0.0 copy-start.14
  60.9 0.0 copy-start.2
  60.9 1.4 copy.37
  62.3 6.2 %all-to-all-start = ((f32[32,8,8,128]{3,2,1,0:T(8,128)}), f32[32,8,8,128]{3,2,1,0:T(8,128)}, u32[]{:S(2)}, u32[]{:S(2)}) async-start(f32[32,8,8,128]{3,2,1,0:T(8,128)} %bitcast.15), calls=%async_computation | async-start | bytes 2097152 | tf_op jit(solution)/shard_map/all_to_all | solution.py:109
  68.5 0.1 fusion.32
  68.6 0.0 collective-permute-done.2
  68.6 0.1 bitcast_add_fusion.1
  68.7 1.7 collective-permute-start.3
  70.4 1.6 convolution_bitcast_fusion.1
  72.0 13.8 %collective-permute-done.3 = f32[4,128,128]{2,1,0:T(8,128)S(1)} collective-permute-done((f32[4,128,128]{2,1,0:T(8,128)S(1)}, f32[4,128,128]{2,1,0:T(8,128)S(1)}, u32[]{:S(2)}, u32[]{:S(2)}) %collective-permute-start.3) | collective-permute-done | bytes 262176 | tf_op jit(solution)/shard_map/ppermute | solution.py:56
  85.9 1.3 collective-permute-start.4
  87.2 0.6 dynamic-slice_bitcast_fusion.1
  87.8 4.9 %collective-permute-done.4 = f32[2,128,128]{2,1,0:T(8,128)S(1)} collective-permute-done((f32[2,128,128]{2,1,0:T(8,128)S(1)}, f32[2,128,128]{2,1,0:T(8,128)S(1)}, u32[]{:S(2)}, u32[]{:S(2)}) %collective-permute-start.4) | collective-permute-done | bytes 131104 | tf_op jit(solution)/shard_map/ppermute | solution.py:56
  92.7 0.6 constant_dynamic-slice_fusion
  93.3 2.5 %collective-permute-start.5 = (f32[1,128,128]{2,1,0:T(8,128)}, f32[1,128,128]{2,1,0:T(8,128)}, u32[]{:S(2)}, u32[]{:S(2)}) collective-permute-start(f32[1,128,128]{2,1,0:T(8,128)} %constant_dynamic-slice_fusion), channel_id=1, source_target_pairs={{0,16},{2,18},{4,20},{6,22},{8,24},{10,26},{12,28},{14,30},{16,0},... | collective-permute-start | bytes 196616 | tf_op jit(solution)/shard_map/ppermute | solution.py:56
  95.8 2.4 %copy.76 = f32[32,8,8,128]{3,1,2,0:T(8,128)} copy(f32[32,8,8,128]{3,2,1,0:T(8,128)} %bitcast.81) | data formatting | bytes 2097152
  98.2 2.5 %copy.39 = f32[1024,256]{1,0:T(8,128)} copy(f32[1024,256]{0,1:T(8,128)} %bitcast.253) | data formatting | bytes 2097152 | tf_op jit(solution)/shard_map/dot_general | solution.py:110
  100.8 2.9 %fusion.50 = f32[16,16,8,128]{3,1,2,0:T(8,128)} fusion(f32[16,16,256,1]{2,1,3,0:T(8,128)} %constant.184, f32[8,128,256,1]{2,1,0,3:T(8,128)} %bitcast.252), kind=kOutput, calls=%fused_computation.118 | convolution fusion | flops 402653184 | bytes 2359296 | tf_op jit(solution)/shard_map/dot_general | solution.py:110
  103.7 4.3 %all-to-all-start.2 = ((f32[16,16,8,128]{3,1,2,0:T(8,128)}), f32[16,16,8,128]{3,1,2,0:T(8,128)}, u32[]{:S(2)}, u32[]{:S(2)}) async-start(f32[16,16,8,128]{3,1,2,0:T(8,128)} %fusion.50), calls=%async_computation.2 | async-start | bytes 2097152 | tf_op jit(solution)/shard_map/all_to_all | solution.py:111
  108.0 1.3 pad_maximum_fusion.1
  109.3 1.5 multiply_bitcast_fusion
  110.8 0.1 fusion.37
  110.9 2.0 convolution_bitcast_fusion.2
  112.9 0.2 copy.48
  113.1 0.3 fusion.48
  113.5 0.0 copy-start.16
  113.5 0.0 copy-start.17
  113.5 0.3 pad_maximum_fusion
  113.9 0.8 copy-done.5
  114.7 0.0 copy-done.16
  114.8 2.5 %fusion.17 = (f32[256,1024]{1,0:T(8,128)S(1)}, f32[1024]{0:T(1024)S(1)}) fusion(f32[32,8,8,128]{3,2,1,0:T(8,128)S(1)} %bitcast.256, f32[256]{0:T(256)S(1)} %copy-done.17, f32[1024]{0:T(1024)S(1)} %bitcast_add_fusion.7, f32[32,8,8,128]{3,2,1,0:T(8,128)S(1)} %bitcast.257, f32[256,256]{1,0:T(8,128)S(1)} %copy-done.16, f32[32,8,8,128]{3,2,1,0:T(8,128)} %all-to-all-done), kind=kOutput, calls=%fused_computation.28 | convolution fusion | flops 406060032 | bytes 4465664 | tf_op jit(solution)/shard_map/dot_general | solution.py:115
  117.3 0.3 multiply_reduce_fusion.1
  117.6 0.1 fusion.43
  117.7 13.2 %all-to-all-done.2 = f32[16,16,8,128]{3,1,2,0:T(8,128)} async-done(((f32[16,16,8,128]{3,1,2,0:T(8,128)}), f32[16,16,8,128]{3,1,2,0:T(8,128)}, u32[]{:S(2)}, u32[]{:S(2)}) %all-to-all-start.2) | async-done | bytes 1048608 | tf_op jit(solution)/shard_map/all_to_all | solution.py:111
  130.9 3.3 %fusion.25 = (f32[16,128,128]{2,1,0:T(8,128)S(1)}, f32[16,128,128]{2,1,0:T(8,128)S(1)}) fusion(f32[1,16,128,128]{3,2,1,0:T(8,128)S(1)} %copy-done, f32[16,16,8,128]{3,0,2,1:T(8,128)} %bitcast.33, f32[16,128,128]{2,1,0:T(8,128)S(1)} %copy-done.3, f32[128,128,1]{1,0,2:T(8,128)S(1)} %copy-done.10), kind=kOutput, calls=%fused_computation.54 | convolution fusion | flops 204472320 | bytes 5308416 | tf_op jit(solution)/shard_map/zxk,ik->zxi/dot_general | solution.py:149
  134.2 3.0 %multiply_reduce_fusion = (f32[128]{0:T(128)S(1)}, f32[128]{0:T(128)S(1)}, f32[128]{0:T(128)S(1)}, f32[128]{0:T(128)S(1)}, f32[128]{0:T(128)S(1)}, /*index=5*/f32[128]{0:T(128)S(1)}, f32[1,16,128,128]{3,2,1,0:T(8,128)}) fusion(f32[16,128,128]{2,1,0:T(8,128)S(1)} %get-tuple-element.40, f32[16,128,128]{2,1,0:T(8,128)S(1)} %get-tuple-element.39, ...), kind=kLoop, calls=%fused_computation.47 | loop fusion | flops 5242112 | bytes 5245952 | tf_op jit(solution)/shard_map/reduce_sum | solution.py:156
  137.3 69.9 %all-gather.1 = f32[32,6,128]{2,1,0:T(8,128)S(1)} all-gather(f32[1,6,128]{2,1,0:T(8,128)S(1)} %bitcast.260), channel_id=2, replica_groups=mesh['band'=16,'spin'=2] {'band','spin'}, dimensions={0}, use_global_device_ids=true | all-gather | bytes 101376 | tf_op jit(solution)/shard_map/all_gather | solution.py:168
  207.2 0.7 reduce_sum.255
  (37 shorter events, 0.2 us)
Async XLA Ops:
  2.9 59.3 %all-to-all-start.1 = ((f32[16,16,8,128]{3,2,1,0:T(8,128)}), f32[16,16,8,128]{3,2,1,0:T(8,128)}, u32[]{:S(2)}, u32[]{:S(2)}) async-start(f32[16,16,8,128]{3,2,1,0:T(8,128)} %copy_bitcast_fusion), calls=%async_computation.1 | async-start | bytes 2097152 | tf_op jit(solution)/shard_map/all_to_all | solution.py:78
  10.4 6.6 %copy-start.15 = (s32[1,2]{1,0:T(1,128)S(1)}, s32[1,2]{1,0:T(1,128)}, u32[]{:S(2)}) copy-start(s32[1,2]{1,0:T(1,128)} %param.17) | copy-start | bytes 28
  40.5 1.6 copy-start
  40.6 3.9 %copy-start.13 = (f32[128]{0:T(128)S(1)}, f32[128]{0:T(128)}, u32[]{:S(2)}) copy-start(f32[128]{0:T(128)} %constant.170.clone) | copy-start | bytes 1540
  40.6 4.2 %copy-start.8 = (s32[3,16384]{1,0:T(4,128)S(1)}, s32[3,16384]{1,0:T(4,128)}, u32[]{:S(2)}) copy-start(s32[3,16384]{1,0:T(4,128)} %param.18) | copy-start | bytes 589828
  41.6 3.9 %collective-permute-start.1 = (f32[8,2,128,128]{3,2,1,0:T(8,128)}, f32[8,2,128,128]{3,2,1,0:T(8,128)}, u32[]{:S(2)}, u32[]{:S(2)}) collective-permute-start(f32[8,2,128,128]{3,2,1,0:T(8,128)} %dynamic-slice_bitcast_fusion.2), channel_id=1, source_target_pairs={{0,2},{2,0},{4,6},{6,4},{8,10},{10,8},{12,14},{14,12},{16,18},{18,... | collective-permute-start | bytes 3145736 | tf_op jit(solution)/shard_map/ppermute | solution.py:56
  43.0 15.1 %collective-permute-start = (f32[8,128,128]{2,1,0:T(8,128)}, f32[8,128,128]{2,1,0:T(8,128)}, u32[]{:S(2)}, u32[]{:S(2)}) collective-permute-start(f32[8,128,128]{2,1,0:T(8,128)} %dynamic-slice_bitcast_fusion.4), channel_id=1, source_target_pairs={{0,1},{1,0},{2,3},{3,2},{4,5},{5,4},{6,7},{7,6},{8,9},{9,8},{10,11... | collective-permute-start | bytes 1572872 | tf_op jit(solution)/shard_map/ppermute | solution.py:81
  45.6 12.6 %copy-start.7 = (f32[2,2,128,128,1]{3,2,1,4,0:T(8,128)S(1)}, f32[2,2,128,128,1]{3,2,1,4,0:T(8,128)}, u32[]{:S(2)}) copy-start(f32[2,2,128,128,1]{3,2,1,4,0:T(8,128)} %constant.181) | copy-start | bytes 786436
  47.0 1.4 copy-start.1
  47.0 13.2 %copy-start.9 = (f32[2,16,8,128,1,1]{3,1,0,2,5,4:T(8,128)S(1)}, f32[2,16,8,128,1,1]{3,1,0,2,5,4:T(8,128)}, u32[]{:S(2)}) copy-start(f32[2,16,8,128,1,1]{3,1,0,2,5,4:T(8,128)} %constant.182) | copy-start | bytes 393220
  47.8 20.8 %collective-permute-start.2 = (f32[8,128,128]{2,1,0:T(8,128)}, f32[8,128,128]{2,1,0:T(8,128)S(1)}, u32[]{:S(2)}, u32[]{:S(2)}) collective-permute-start(f32[8,128,128]{2,1,0:T(8,128)} %dynamic-slice_bitcast_fusion.3), channel_id=1, source_target_pairs={{0,1},{1,0},{2,3},{3,2},{4,5},{5,4},{6,7},{7,6},{8,9},{9,8},{10,11... | collective-permute-start | bytes 1572872 | tf_op jit(solution)/shard_map/ppermute | solution.py:61
  60.9 7.6 %copy-start.6 = (f32[1,3,128,128]{3,1,2,0:T(4,128)S(1)}, f32[1,3,128,128]{3,1,2,0:T(4,128)}, u32[]{:S(2)}) copy-start(f32[1,3,128,128]{3,1,2,0:T(4,128)} %convert_bitcast_fusion) | copy-start | bytes 589828
  60.9 7.6 %copy-start.14 = (f32[3]{0:T(128)S(1)}, f32[3]{0:T(128)}, u32[]{:S(2)}) copy-start(f32[3]{0:T(128)} %constant.172.clone) | copy-start | bytes 40
  60.9 7.7 %copy-start.2 = (f32[8,2,128,128]{3,2,1,0:T(8,128)S(1)}, f32[8,2,128,128]{3,2,1,0:T(8,128)}, u32[]{:S(2)}) copy-start(f32[8,2,128,128]{3,2,1,0:T(8,128)} %copy-done.1) | copy-start | bytes 3145732
  62.3 8.2 %copy-start.10 = (f32[128,128,1]{1,0,2:T(8,128)S(1)}, f32[128,128,1]{1,0,2:T(8,128)}, u32[]{:S(2)}) copy-start(f32[128,128,1]{1,0,2:T(8,128)} %constant.183) | copy-start | bytes 196612
  62.3 41.4 %all-to-all-start = ((f32[32,8,8,128]{3,2,1,0:T(8,128)}), f32[32,8,8,128]{3,2,1,0:T(8,128)}, u32[]{:S(2)}, u32[]{:S(2)}) async-start(f32[32,8,8,128]{3,2,1,0:T(8,128)} %bitcast.15), calls=%async_computation | async-start | bytes 2097152 | tf_op jit(solution)/shard_map/all_to_all | solution.py:109
  68.7 18.5 %copy-start.4 = (f32[2,256,8,128]{3,2,1,0:T(8,128)S(1)}, f32[2,256,8,128]{3,2,1,0:T(8,128)}, u32[]{:S(2)}) copy-start(f32[2,256,8,128]{3,2,1,0:T(8,128)} %param.20) | copy-start | bytes 6291460
  68.7 17.1 %collective-permute-start.3 = (f32[4,128,128]{2,1,0:T(8,128)S(1)}, f32[4,128,128]{2,1,0:T(8,128)S(1)}, u32[]{:S(2)}, u32[]{:S(2)}) collective-permute-start(f32[4,128,128]{2,1,0:T(8,128)S(1)} %dynamic-slice_bitcast_fusion.5), channel_id=1, source_target_pairs={{0,4},{2,6},{4,0},{6,2},{8,12},{10,14},{12,8},{14,10},{16,20},{18,... | collective-permute-start | bytes 786440 | tf_op jit(solution)/shard_map/ppermute | solution.py:56
  85.9 6.8 %collective-permute-start.4 = (f32[2,128,128]{2,1,0:T(8,128)S(1)}, f32[2,128,128]{2,1,0:T(8,128)S(1)}, u32[]{:S(2)}, u32[]{:S(2)}) collective-permute-start(f32[2,128,128]{2,1,0:T(8,128)S(1)} %dynamic-slice_bitcast_fusion.6), channel_id=1, source_target_pairs={{0,8},{2,10},{4,12},{6,14},{8,0},{10,2},{12,4},{14,6},{16,24},{18,... | collective-permute-start | bytes 393224 | tf_op jit(solution)/shard_map/ppermute | solution.py:56
  93.3 16.0 %collective-permute-start.5 = (f32[1,128,128]{2,1,0:T(8,128)}, f32[1,128,128]{2,1,0:T(8,128)}, u32[]{:S(2)}, u32[]{:S(2)}) collective-permute-start(f32[1,128,128]{2,1,0:T(8,128)} %constant_dynamic-slice_fusion), channel_id=1, source_target_pairs={{0,16},{2,18},{4,20},{6,22},{8,24},{10,26},{12,28},{14,30},{16,0},... | collective-permute-start | bytes 196616 | tf_op jit(solution)/shard_map/ppermute | solution.py:56
  103.7 27.2 %all-to-all-start.2 = ((f32[16,16,8,128]{3,1,2,0:T(8,128)}), f32[16,16,8,128]{3,1,2,0:T(8,128)}, u32[]{:S(2)}, u32[]{:S(2)}) async-start(f32[16,16,8,128]{3,1,2,0:T(8,128)} %fusion.50), calls=%async_computation.2 | async-start | bytes 2097152 | tf_op jit(solution)/shard_map/all_to_all | solution.py:111
  113.5 1.2 copy-start.5
  113.5 1.3 copy-start.16
  113.5 1.2 copy-start.17
  114.8 2.6 %copy-start.11 = (f32[256]{0:T(256)S(1)}, f32[256]{0:T(256)}, u32[]{:S(2)}) copy-start(f32[256]{0:T(256)} %constant.179) | copy-start | bytes 3076
  114.8 2.6 %copy-start.12 = (f32[256]{0:T(256)S(1)}, f32[256]{0:T(256)}, u32[]{:S(2)}) copy-start(f32[256]{0:T(256)} %constant.180) | copy-start | bytes 3076
  114.8 16.1 %copy-start.3 = (f32[16,128,128]{2,1,0:T(8,128)S(1)}, f32[16,128,128]{2,1,0:T(8,128)}, u32[]{:S(2)}) copy-start(f32[16,128,128]{2,1,0:T(8,128)} %convolution_bitcast_fusion.1) | copy-start | bytes 3145732
